TPU v7x, 32 devices: a whole 2x2x4 slice. The times are simulated.
32 devices in a mesh: grp: 2 (over y), lat: 4 (over z), lon: 2 (over x), ch: 2 (over core).
Axes of the slice: x: 2, y: 2, z: 4, core: 2. Of those that a mesh axis runs over, the one named last changes fastest.
Arguments:
- noisy_state: bfloat16 [256, 32, 512], P(('grp', 'ch'), 'lat', 'lon'), parts along dimension 0, may hold values from -6 to 6
- kernel_in: bfloat16 [3, 3, 128, 128], replicated, may hold values from -0.1875 to 0.1875
- bias_in: float32 [128], replicated, may hold values from -4 to 4
- kernel_out: bfloat16 [3, 3, 128, 128], replicated, may hold values from -0.1875 to 0.1875
- interp_weight: bfloat16 [64, 128, 128], P(('grp', 'lat', 'lon')), parts along dimension 0, may hold values from -0.5 to 0.5
- observed: bfloat16 [64, 128, 128], P(('grp', 'lat', 'lon'), 'ch'), parts along dimension 0, may hold values from -6 to 6
- obs_precision: bfloat16 [64, 128], P(('grp', 'lat', 'lon')), parts along dimension 0, may hold values from 0.29882812 to 3
- dest_tile: int32 [64], P(('grp', 'lat', 'lon')), parts along dimension 0, may hold values from 0 to 3, as said below
- row_offset: int32 [64], P(('grp', 'lat', 'lon')), parts along dimension 0, may hold values from 0 to 4
- col_offset: int32 [64], P(('grp', 'lat', 'lon')), parts along dimension 0, may hold values from 0 to 224
Outputs:
- next_state: float32 [256, 32, 512], P(('grp', 'ch'), 'lat', 'lon'), parts along dimension 0
- innovation: bfloat16 [64, 128, 128], P(('grp', 'lat', 'lon'), 'ch'), parts along dimension 0
There are 2 independent parts, one for each index of `grp`. A program takes and returns all parts, laid end to end along the dimension named above; an argument that names none is the same for every part. Nothing has to cross between parts.
Inputs may be any that keep to these rules, and one draw needn't show every extreme that they name: `dest_tile`: the 4 blocks of one device name any one latitude tile at most 2 times; a block's tile lies in the longitude column of the device that holds the block.
All inputs are finite; a program needn't handle non-finite values.
Results may differ from a plain program's by a relative error of at most 0.0085.
Values may be sent and summed in bfloat16 or wider, within the bound.
No kernel may reach another device: no remote copies, remote signals or barrier semaphores. Data moves between devices by JAX's collectives and lax.ppermute only.
A program may use at most 64 MiB of HBM per device.

v0:
```python
import jax
import jax.numpy as jnp
from jax import lax
from jax.sharding import PartitionSpec as P

OBS = 128
PH = 4
PW = 32
CAP = 2
keep_rate = 0.6
blend_rate = 0.4
guide_rate = 0.3


def extended(shard, sides, width):
    for axis, dim in sides:
        size, length = (lax.axis_size(axis), shard.shape[dim])
        up = [(i, (i + 1) % size) for i in range(size)]
        down = [(j, i) for i, j in up]
        last = lax.slice_in_dim(shard, length - width, length, axis=dim)
        initial = lax.slice_in_dim(shard, 0, width, axis=dim)
        before = lax.ppermute(last, axis, up)
        after = lax.ppermute(initial, axis, down)
        shard = jnp.concatenate([before, shard, after], axis=dim)
    return shard


def with_rims(grid_field):
    padded = extended(grid_field, (("lat", 1), ("lon", 2)), 1)
    position = lax.axis_index("lat")
    lat_count = lax.axis_size("lat")
    levels = lax.broadcasted_iota(jnp.int32, (1, padded.shape[1], 1), 1)
    inside = ((levels > 0) | (position > 0)) & (
        (levels < padded.shape[1] - 1) | (position < lat_count - 1)
    )
    return jnp.where(inside, padded, jnp.zeros((), padded.dtype))


def apply_taps(running, kernel_part, padded, grid_rows, grid_cols):
    in_count = padded.shape[0]
    out_count = kernel_part.shape[2]
    for tap_row in range(3):
        stacked = jnp.concatenate(
            [
                padded[:, tap_row : tap_row + grid_rows, tap_col : tap_col + grid_cols]
                for tap_col in range(3)
            ],
            axis=0,
        )
        row_kernel = jnp.transpose(kernel_part[tap_row], (1, 0, 2)).reshape(out_count, 3 * in_count)
        running = running + jnp.einsum(
            "oi,ihw->ohw", row_kernel, stacked, preferred_element_type=jnp.float32
        )
    return running


def convolve(grid_field, kernel_rows):
    padded = with_rims(grid_field)
    grid_rows, grid_cols = (grid_field.shape[1], grid_field.shape[2])
    initial = jnp.zeros((kernel_rows.shape[2], grid_rows, grid_cols), jnp.float32)
    return apply_taps(
        initial, kernel_rows, lax.all_gather(padded, "ch", axis=0, tiled=True), grid_rows, grid_cols
    )


def forward_rows(kernel, first_channel, own_channels):
    return lax.dynamic_slice_in_dim(kernel, first_channel, own_channels, 2)


def adjoint_rows(kernel, first_channel, own_channels):
    columns = lax.dynamic_slice_in_dim(kernel, first_channel, own_channels, 3)
    return jnp.transpose(columns[::-1, ::-1], (0, 1, 3, 2))


def extract(grid_field, patch_rows, patch_cols):

    def take_one(row_start, col_start):
        return lax.dynamic_slice(
            grid_field,
            (jnp.zeros((), jnp.int32), row_start, col_start),
            (grid_field.shape[0], PH, PW),
        )

    return jax.vmap(take_one)(patch_rows, patch_cols)


def spread(grad_patch, patch_rows, patch_cols, grid_shape):
    cell_rows = patch_rows[:, None, None] + lax.broadcasted_iota(jnp.int32, (1, PH, 1), 1)
    cell_cols = patch_cols[:, None, None] + lax.broadcasted_iota(jnp.int32, (1, 1, PW), 2)
    return (
        jnp.zeros(grid_shape, jnp.float32)
        .at[:, cell_rows, cell_cols]
        .add(jnp.moveaxis(grad_patch, 1, 0))
    )


def slot_plan(dest_tile, lat_tiles):
    blocks = dest_tile.shape[0]
    matches = (dest_tile[:, None] == lax.broadcasted_iota(jnp.int32, (1, lat_tiles), 1)).astype(
        jnp.int32
    )
    before = jnp.cumsum(matches, axis=0) - matches
    slot_rank = jnp.sum(before * matches, axis=1)
    flat_slot = dest_tile * CAP + slot_rank
    filler = (
        jnp.full((lat_tiles * CAP,), blocks, jnp.int32)
        .at[flat_slot]
        .set(lax.iota(jnp.int32, blocks))
    )
    filled = filler < blocks
    source = jnp.minimum(filler, blocks - 1)
    return (flat_slot, source, filled)


def observe(denoised, interp_weight, observed, obs_precision, dest_tile, row_offset, col_offset):
    own_channels = denoised.shape[0]
    grid_shape = denoised.shape
    lat_tiles = lax.axis_size("lat")
    slots = lat_tiles * CAP
    flat_slot, source, filled = slot_plan(dest_tile, lat_tiles)
    rows_out = row_offset[source].reshape(lat_tiles, CAP)
    cols_out = col_offset[source].reshape(lat_tiles, CAP)
    weights_out = jnp.where(
        filled[:, None, None], interp_weight[source], jnp.zeros((), jnp.bfloat16)
    ).reshape(lat_tiles, CAP, OBS, PH * PW)
    values_out = observed[source].reshape(lat_tiles, CAP, own_channels, OBS)
    scale_out = jnp.where(
        filled[:, None], obs_precision[source], jnp.zeros((), jnp.bfloat16)
    ).reshape(lat_tiles, CAP, OBS)
    arrived = (
        lax.all_to_all(weights_out, "lat", split_axis=0, concat_axis=0, tiled=True),
        lax.all_to_all(values_out, "lat", split_axis=0, concat_axis=0, tiled=True),
        lax.all_to_all(scale_out, "lat", split_axis=0, concat_axis=0, tiled=True),
        lax.all_to_all(rows_out, "lat", split_axis=0, concat_axis=0, tiled=True),
        lax.all_to_all(cols_out, "lat", split_axis=0, concat_axis=0, tiled=True),
    )
    weights_in = arrived[0].reshape(slots, OBS, PH * PW)
    values_in = arrived[1].reshape(slots, own_channels, OBS)
    scale_in = arrived[2].reshape(slots, OBS)
    rows_in = arrived[3].reshape(slots)
    cols_in = arrived[4].reshape(slots)
    patches = extract(denoised, rows_in, cols_in).reshape(slots, own_channels, PH * PW)
    predicted = jnp.einsum("scp,sop->sco", patches, weights_in, preferred_element_type=jnp.float32)
    residual = predicted - values_in.astype(jnp.float32)
    rounded = residual.astype(jnp.bfloat16).reshape(lat_tiles, CAP, own_channels, OBS)
    returned = lax.all_to_all(rounded, "lat", split_axis=0, concat_axis=0, tiled=True).reshape(
        slots, own_channels, OBS
    )
    innovation = returned[flat_slot]
    weighted = (residual * scale_in.astype(jnp.float32)[:, None, :]).astype(jnp.bfloat16)
    pulled = jnp.einsum("sco,sop->scp", weighted, weights_in, preferred_element_type=jnp.float32)
    grad_field = spread(pulled.reshape(slots, own_channels, PH, PW), rows_in, cols_in, grid_shape)
    return (grad_field, innovation)


def body(
    noisy_state,
    kernel_in,
    bias_in,
    kernel_out,
    interp_weight,
    observed,
    obs_precision,
    dest_tile,
    row_offset,
    col_offset,
):
    own_channels = noisy_state.shape[0]
    first_channel = lax.axis_index("ch") * own_channels
    bias_local = lax.dynamic_slice_in_dim(bias_in, first_channel, own_channels, 0)
    pre_act = (
        convolve(noisy_state, forward_rows(kernel_in, first_channel, own_channels))
        + bias_local[:, None, None]
    )
    hidden = jax.nn.silu(pre_act).astype(jnp.bfloat16)
    denoised = (
        noisy_state.astype(jnp.float32)
        + convolve(hidden, forward_rows(kernel_out, first_channel, own_channels))
    ).astype(jnp.bfloat16)
    grad_field, innovation = observe(
        denoised, interp_weight, observed, obs_precision, dest_tile, row_offset, col_offset
    )
    grad_round = grad_field.astype(jnp.bfloat16)
    back_hidden = convolve(grad_round, adjoint_rows(kernel_out, first_channel, own_channels))
    sigmoid_act = jax.nn.sigmoid(pre_act)
    grad_pre = (back_hidden * sigmoid_act * (1.0 + pre_act * (1.0 - sigmoid_act))).astype(
        jnp.bfloat16
    )
    grad_state = grad_field + convolve(
        grad_pre, adjoint_rows(kernel_in, first_channel, own_channels)
    )
    next_state = (
        keep_rate * noisy_state.astype(jnp.float32)
        + blend_rate * denoised.astype(jnp.float32)
        - guide_rate * grad_state
    )
    return (next_state, innovation)


def solution(mesh):
    return jax.shard_map(
        body,
        mesh=mesh,
        in_specs=(
            P(("grp", "ch"), "lat", "lon"),
            P(),
            P(),
            P(),
            P(("grp", "lat", "lon"), None, None),
            P(("grp", "lat", "lon"), "ch", None),
            P(("grp", "lat", "lon"), None),
            P(("grp", "lat", "lon")),
            P(("grp", "lat", "lon")),
            P(("grp", "lat", "lon")),
        ),
        out_specs=(P(("grp", "ch"), "lat", "lon"), P(("grp", "lat", "lon"), "ch", None)),
        check_vma=False,
    )
```

profile of v0, /device:TPU:0, one launch (start us, length us, event | category | flops | bytes accessed | tf_op | source)
XLA Modules:
  0.0 143.8 jit_solution(14844164952837276044)
XLA Ops:
  1.9 3.1 %collective-permute-start = (bf16[64,1,256]{2,0,1:T(8,128)(2,1)S(1)}, bf16[64,1,256]{2,0,1:T(8,128)(2,1)S(1)}, u32[]{:S(2)}, u32[]{:S(2)}) collective-permute-start(bf16[64,1,256]{2,0,1:T(8,128)(2,1)S(1)} %copy.179), channel_id=1, source_target_pairs={{0,4},{4,8},{8,12},{12,0},{1,5},{5,9},{9,13},{13,1},{2,6},{6,10},{... | collective-permute-start | bytes 98312 | tf_op jit(solution)/shard_map/ppermute | solution.py:22
  5.0 2.1 %collective-permute-start.1 = (bf16[64,1,256]{2,0,1:T(8,128)(2,1)S(1)}, bf16[64,1,256]{2,0,1:T(8,128)(2,1)S(1)}, u32[]{:S(2)}, u32[]{:S(2)}) collective-permute-start(bf16[64,1,256]{2,0,1:T(8,128)(2,1)S(1)} %copy.180), channel_id=1, source_target_pairs={{4,0},{8,4},{12,8},{0,12},{5,1},{9,5},{13,9},{1,13},{6,2},{10,6},{... | collective-permute-start | bytes 98312 | tf_op jit(solution)/shard_map/ppermute | solution.py:23
  12.0 3.2 %all-to-all-start.1 = ((s32[4,1,2]{2,1,0:T(1,128)}), s32[4,1,2]{2,1,0:T(1,128)S(1)}, u32[]{:S(2)}, u32[]{:S(2)}) async-start(s32[4,1,2]{2,1,0:T(1,128)} %bitcast.13), calls=%async_computation.1 | async-start | bytes 4096 | tf_op jit(solution)/shard_map/all_to_all | solution.py:135
  21.6 5.1 %all-to-all-start = ((s32[4,1,2]{2,1,0:T(1,128)}), s32[4,1,2]{2,1,0:T(1,128)S(1)}, u32[]{:S(2)}, u32[]{:S(2)}) async-start(s32[4,1,2]{2,1,0:T(1,128)} %bitcast.12), calls=%async_computation | async-start | bytes 4096 | tf_op jit(solution)/shard_map/all_to_all | solution.py:134
  28.0 4.2 %all-to-all-done = s32[4,1,2]{2,1,0:T(1,128)S(1)} async-done(((s32[4,1,2]{2,1,0:T(1,128)}), s32[4,1,2]{2,1,0:T(1,128)S(1)}, u32[]{:S(2)}, u32[]{:S(2)}) %all-to-all-start) | async-done | bytes 64 | tf_op jit(solution)/shard_map/all_to_all | solution.py:134
  32.2 3.2 %all-to-all-start.4 = ((bf16[4,2,128]{2,1,0:T(2,128)(2,1)}), bf16[4,2,128]{2,1,0:T(2,128)(2,1)S(1)}, u32[]{:S(2)}, u32[]{:S(2)}) async-start(bf16[4,2,128]{2,1,0:T(2,128)(2,1)} %broadcast_select_fusion.2), calls=%async_computation.4 | async-start | bytes 4096 | tf_op jit(solution)/shard_map/all_to_all | solution.py:133
  38.9 3.5 %collective-permute-done.2 = bf16[64,10,1]{2,0,1:T(8,128)(2,1)S(1)} collective-permute-done((bf16[64,10,1]{2,0,1:T(8,128)(2,1)S(1)}, bf16[64,10,1]{2,0,1:T(8,128)(2,1)S(1)}, u32[]{:S(2)}, u32[]{:S(2)}) %collective-permute-start.2) | collective-permute-done | bytes 1312 | tf_op jit(solution)/shard_map/ppermute | solution.py:22
  42.4 1.8 %collective-permute-done.3 = bf16[64,10,1]{2,0,1:T(8,128)(2,1)S(1)} collective-permute-done((bf16[64,10,1]{2,0,1:T(8,128)(2,1)S(1)}, bf16[64,10,1]{2,0,1:T(8,128)(2,1)S(1)}, u32[]{:S(2)}, u32[]{:S(2)}) %collective-permute-start.3) | collective-permute-done | bytes 1312 | tf_op jit(solution)/shard_map/ppermute | solution.py:23
  44.5 2.5 %all_gather.12 = bf16[128,10,258]{2,0,1:T(8,128)(2,1)S(1)} all-gather(bf16[64,10,258]{2,0,1:T(8,128)(2,1)S(1)} %maximum_select_fusion), channel_id=1, replica_groups=mesh['grp'=2,'lat'=4,'lon'=2,'ch'=2] {'ch'}, dimensions={0}, use_global_device_ids=true | all-gather | bytes 990720 | tf_op jit(solution)/shard_map/all_gather | solution.py:62
  51.9 2.1 %collective-permute-start.5 = (bf16[64,1,256]{2,0,1:T(8,128)(2,1)S(1)}, bf16[64,1,256]{2,0,1:T(8,128)(2,1)S(1)}, u32[]{:S(2)}, u32[]{:S(2)}) collective-permute-start(bf16[64,1,256]{2,0,1:T(8,128)(2,1)S(1)} %get-tuple-element.117), channel_id=1, source_target_pairs={{4,0},{8,4},{12,8},{0,12},{5,1},{9,5},{13,9},{1,13},{6,2},{10,6},{... | collective-permute-start | bytes 98312 | tf_op jit(solution)/shard_map/ppermute | solution.py:23
  54.1 2.0 %collective-permute-done.4 = bf16[64,1,256]{2,0,1:T(8,128)(2,1)S(1)} collective-permute-done((bf16[64,1,256]{2,0,1:T(8,128)(2,1)S(1)}, bf16[64,1,256]{2,0,1:T(8,128)(2,1)S(1)}, u32[]{:S(2)}, u32[]{:S(2)}) %collective-permute-start.4) | collective-permute-done | bytes 32800 | tf_op jit(solution)/shard_map/ppermute | solution.py:22
  58.6 4.8 %all-to-all-start.3 = ((bf16[4,2,64,128]{3,2,1,0:T(8,128)(2,1)}), bf16[4,2,64,128]{3,2,1,0:T(8,128)(2,1)S(1)}, u32[]{:S(2)}, u32[]{:S(2)}) async-start(bf16[4,2,64,128]{3,2,1,0:T(8,128)(2,1)} %bitcast.17), calls=%async_computation.3 | async-start | bytes 262144 | tf_op jit(solution)/shard_map/all_to_all | solution.py:132
  65.1 2.5 %all_gather.13 = bf16[128,10,258]{2,0,1:T(8,128)(2,1)S(1)} all-gather(bf16[64,10,258]{2,0,1:T(8,128)(2,1)S(1)} %maximum_select_fusion.1), channel_id=1, replica_groups=mesh['grp'=2,'lat'=4,'lon'=2,'ch'=2] {'ch'}, dimensions={0}, use_global_device_ids=true | all-gather | bytes 990720 | tf_op jit(solution)/shard_map/all_gather | solution.py:62
  70.1 4.8 %all-to-all-start.2 = ((bf16[4,2,128,128]{3,2,1,0:T(8,128)(2,1)}), bf16[4,2,128,128]{3,2,1,0:T(8,128)(2,1)S(1)}, u32[]{:S(2)}, u32[]{:S(2)}) async-start(bf16[4,2,128,128]{3,2,1,0:T(8,128)(2,1)} %broadcast_select_fusion), calls=%async_computation.2 | async-start | bytes 524288 | tf_op jit(solution)/shard_map/all_to_all | solution.py:131
  74.9 18.2 %while.1 = (s32[]{:T(128)}, bf16[64,8,256]{2,0,1:T(8,128)(2,1)S(1)}, s32[8,3]{0,1:T(4,128)S(1)}, bf16[8,64,4,32]{1,3,2,0:T(8,128)(2,1)S(1)}, s32[]{:T(128)}) while((s32[]{:T(128)}, bf16[64,8,256]{2,0,1:T(8,128)(2,1)S(1)}, s32[8,3]{0,1:T(4,128)S(1)}, bf16[8,64,4,32]{1,3,2,0:T(8,128)(2,1)S(1)}, s32[]{:T(128)}) %tuple.87), condition=%wide.while_cond, body=%wide.while_body.sunk | while | flops 2 | bytes 163957 | solution.py:78
  94.3 6.3 %scatter_custom_fusion.1 = f32[64,2048]{0,1:T(8,128)S(1)} fusion(s32[1024]{0:T(1024)S(1)} %reshape.338, f32[1024,64]{1,0:T(8,128)S(1)} %bitcast.128, f32[]{:T(128)} %constant.30.clone.1), kind=kCustom, calls=%fused_computation.104 | custom fusion | flops 65536 | bytes 524292
  101.0 2.1 %collective-permute-start.8 = (bf16[64,1,256]{2,0,1:T(8,128)(2,1)S(1)}, bf16[64,1,256]{2,0,1:T(8,128)(2,1)S(1)}, u32[]{:S(2)}, u32[]{:S(2)}) collective-permute-start(bf16[64,1,256]{2,0,1:T(8,128)(2,1)S(1)} %get-tuple-element.114), channel_id=1, source_target_pairs={{0,4},{4,8},{8,12},{12,0},{1,5},{5,9},{9,13},{13,1},{2,6},{6,10},{... | collective-permute-start | bytes 98312 | tf_op jit(solution)/shard_map/ppermute | solution.py:22
  103.1 2.0 %collective-permute-start.9 = (bf16[64,1,256]{2,0,1:T(8,128)(2,1)S(1)}, bf16[64,1,256]{2,0,1:T(8,128)(2,1)S(1)}, u32[]{:S(2)}, u32[]{:S(2)}) collective-permute-start(bf16[64,1,256]{2,0,1:T(8,128)(2,1)S(1)} %get-tuple-element.115), channel_id=1, source_target_pairs={{4,0},{8,4},{12,8},{0,12},{5,1},{9,5},{13,9},{1,13},{6,2},{10,6},{... | collective-permute-start | bytes 98312 | tf_op jit(solution)/shard_map/ppermute | solution.py:23
  109.4 4.2 %collective-permute-done.10 = bf16[64,10,1]{2,0,1:T(8,128)(2,1)S(1)} collective-permute-done((bf16[64,10,1]{2,0,1:T(8,128)(2,1)S(1)}, bf16[64,10,1]{2,0,1:T(8,128)(2,1)S(1)}, u32[]{:S(2)}, u32[]{:S(2)}) %collective-permute-start.10) | collective-permute-done | bytes 1312 | tf_op jit(solution)/shard_map/ppermute | solution.py:22
  115.7 2.5 %all_gather.14 = bf16[128,10,258]{2,0,1:T(8,128)(2,1)S(1)} all-gather(bf16[64,10,258]{2,0,1:T(8,128)(2,1)S(1)} %maximum_select_fusion.2), channel_id=1, replica_groups=mesh['grp'=2,'lat'=4,'lon'=2,'ch'=2] {'ch'}, dimensions={0}, use_global_device_ids=true | all-gather | bytes 990720 | tf_op jit(solution)/shard_map/all_gather | solution.py:62
  122.8 2.4 %collective-permute-start.13 = (bf16[64,1,256]{2,0,1:T(8,128)(2,1)S(1)}, bf16[64,1,256]{2,0,1:T(8,128)(2,1)S(1)}, u32[]{:S(2)}, u32[]{:S(2)}) collective-permute-start(bf16[64,1,256]{2,0,1:T(8,128)(2,1)S(1)} %get-tuple-element.113), channel_id=1, source_target_pairs={{4,0},{8,4},{12,8},{0,12},{5,1},{9,5},{13,9},{1,13},{6,2},{10,6},{... | collective-permute-start | bytes 98312 | tf_op jit(solution)/shard_map/ppermute | solution.py:23
  125.3 1.9 %collective-permute-done.12 = bf16[64,1,256]{2,0,1:T(8,128)(2,1)S(1)} collective-permute-done((bf16[64,1,256]{2,0,1:T(8,128)(2,1)S(1)}, bf16[64,1,256]{2,0,1:T(8,128)(2,1)S(1)}, u32[]{:S(2)}, u32[]{:S(2)}) %collective-permute-start.12) | collective-permute-done | bytes 32800 | tf_op jit(solution)/shard_map/ppermute | solution.py:22
  129.5 5.0 %all-to-all-start.5 = ((bf16[4,2,64,128]{3,2,1,0:T(8,128)(2,1)}), bf16[4,2,64,128]{3,2,1,0:T(8,128)(2,1)S(1)}, u32[]{:S(2)}, u32[]{:S(2)}) async-start(bf16[4,2,64,128]{3,2,1,0:T(8,128)(2,1)} %bitcast.51), calls=%async_computation.5 | async-start | bytes 262144 | tf_op jit(solution)/shard_map/all_to_all | solution.py:146
  136.5 2.5 %all_gather.15 = bf16[128,10,258]{2,0,1:T(8,128)(2,1)S(1)} all-gather(bf16[64,10,258]{2,0,1:T(8,128)(2,1)S(1)} %maximum_select_fusion.3), channel_id=1, replica_groups=mesh['grp'=2,'lat'=4,'lon'=2,'ch'=2] {'ch'}, dimensions={0}, use_global_device_ids=true | all-gather | bytes 990720 | tf_op jit(solution)/shard_map/all_gather | solution.py:62
  (200 shorter events, 68.5 us)
Async XLA Ops:
  1.9 34.5 %collective-permute-start = (bf16[64,1,256]{2,0,1:T(8,128)(2,1)S(1)}, bf16[64,1,256]{2,0,1:T(8,128)(2,1)S(1)}, u32[]{:S(2)}, u32[]{:S(2)}) collective-permute-start(bf16[64,1,256]{2,0,1:T(8,128)(2,1)S(1)} %copy.179), channel_id=1, source_target_pairs={{0,4},{4,8},{8,12},{12,0},{1,5},{5,9},{9,13},{13,1},{2,6},{6,10},{... | collective-permute-start | bytes 98312 | tf_op jit(solution)/shard_map/ppermute | solution.py:22
  5.0 31.5 %collective-permute-start.1 = (bf16[64,1,256]{2,0,1:T(8,128)(2,1)S(1)}, bf16[64,1,256]{2,0,1:T(8,128)(2,1)S(1)}, u32[]{:S(2)}, u32[]{:S(2)}) collective-permute-start(bf16[64,1,256]{2,0,1:T(8,128)(2,1)S(1)} %copy.180), channel_id=1, source_target_pairs={{4,0},{8,4},{12,8},{0,12},{5,1},{9,5},{13,9},{1,13},{6,2},{10,6},{... | collective-permute-start | bytes 98312 | tf_op jit(solution)/shard_map/ppermute | solution.py:23
  12.0 9.7 %all-to-all-start.1 = ((s32[4,1,2]{2,1,0:T(1,128)}), s32[4,1,2]{2,1,0:T(1,128)S(1)}, u32[]{:S(2)}, u32[]{:S(2)}) async-start(s32[4,1,2]{2,1,0:T(1,128)} %bitcast.13), calls=%async_computation.1 | async-start | bytes 4096 | tf_op jit(solution)/shard_map/all_to_all | solution.py:135
  17.0 19.3 %copy-start.8 = (s32[2]{0:T(128)S(1)}, s32[2]{0:T(128)}, u32[]{:S(2)}) copy-start(s32[2]{0:T(128)} %constant.64) | copy-start | bytes 28
  17.0 19.4 %copy-start.7 = (s32[2]{0:T(128)S(1)}, s32[2]{0:T(128)}, u32[]{:S(2)}) copy-start(s32[2]{0:T(128)} %constant.61) | copy-start | bytes 28
  21.6 10.6 %all-to-all-start = ((s32[4,1,2]{2,1,0:T(1,128)}), s32[4,1,2]{2,1,0:T(1,128)S(1)}, u32[]{:S(2)}, u32[]{:S(2)}) async-start(s32[4,1,2]{2,1,0:T(1,128)} %bitcast.12), calls=%async_computation | async-start | bytes 4096 | tf_op jit(solution)/shard_map/all_to_all | solution.py:134
  32.2 26.4 %all-to-all-start.4 = ((bf16[4,2,128]{2,1,0:T(2,128)(2,1)}), bf16[4,2,128]{2,1,0:T(2,128)(2,1)S(1)}, u32[]{:S(2)}, u32[]{:S(2)}) async-start(bf16[4,2,128]{2,1,0:T(2,128)(2,1)} %broadcast_select_fusion.2), calls=%async_computation.4 | async-start | bytes 4096 | tf_op jit(solution)/shard_map/all_to_all | solution.py:133
  36.7 5.7 %collective-permute-start.2 = (bf16[64,10,1]{2,0,1:T(8,128)(2,1)S(1)}, bf16[64,10,1]{2,0,1:T(8,128)(2,1)S(1)}, u32[]{:S(2)}, u32[]{:S(2)}) collective-permute-start(bf16[64,10,1]{2,0,1:T(8,128)(2,1)S(1)} %get-tuple-element.98), channel_id=1, source_target_pairs={{0,2},{2,0},{1,3},{3,1},{4,6},{6,4},{5,7},{7,5},{8,10},{10,8},{9,1... | collective-permute-start | bytes 3848 | tf_op jit(solution)/shard_map/ppermute | solution.py:22
  38.3 5.8 %collective-permute-start.3 = (bf16[64,10,1]{2,0,1:T(8,128)(2,1)S(1)}, bf16[64,10,1]{2,0,1:T(8,128)(2,1)S(1)}, u32[]{:S(2)}, u32[]{:S(2)}) collective-permute-start(bf16[64,10,1]{2,0,1:T(8,128)(2,1)S(1)} %get-tuple-element.99), channel_id=1, source_target_pairs={{2,0},{0,2},{3,1},{1,3},{6,4},{4,6},{7,5},{5,7},{10,8},{8,10},{11,... | collective-permute-start | bytes 3848 | tf_op jit(solution)/shard_map/ppermute | solution.py:23
  50.2 5.8 %collective-permute-start.4 = (bf16[64,1,256]{2,0,1:T(8,128)(2,1)S(1)}, bf16[64,1,256]{2,0,1:T(8,128)(2,1)S(1)}, u32[]{:S(2)}, u32[]{:S(2)}) collective-permute-start(bf16[64,1,256]{2,0,1:T(8,128)(2,1)S(1)} %get-tuple-element.116), channel_id=1, source_target_pairs={{0,4},{4,8},{8,12},{12,0},{1,5},{5,9},{9,13},{13,1},{2,6},{6,10},{... | collective-permute-start | bytes 98312 | tf_op jit(solution)/shard_map/ppermute | solution.py:22
  51.9 4.3 %collective-permute-start.5 = (bf16[64,1,256]{2,0,1:T(8,128)(2,1)S(1)}, bf16[64,1,256]{2,0,1:T(8,128)(2,1)S(1)}, u32[]{:S(2)}, u32[]{:S(2)}) collective-permute-start(bf16[64,1,256]{2,0,1:T(8,128)(2,1)S(1)} %get-tuple-element.117), channel_id=1, source_target_pairs={{4,0},{8,4},{12,8},{0,12},{5,1},{9,5},{13,9},{1,13},{6,2},{10,6},{... | collective-permute-start | bytes 98312 | tf_op jit(solution)/shard_map/ppermute | solution.py:23
  56.4 7.1 %collective-permute-start.6 = (bf16[64,10,1]{2,0,1:T(8,128)(2,1)S(1)}, bf16[64,10,1]{2,0,1:T(8,128)(2,1)S(1)}, u32[]{:S(2)}, u32[]{:S(2)}) collective-permute-start(bf16[64,10,1]{2,0,1:T(8,128)(2,1)S(1)} %get-tuple-element.96), channel_id=1, source_target_pairs={{0,2},{2,0},{1,3},{3,1},{4,6},{6,4},{5,7},{7,5},{8,10},{10,8},{9,1... | collective-permute-start | bytes 3848 | tf_op jit(solution)/shard_map/ppermute | solution.py:22
  58.0 6.8 %collective-permute-start.7 = (bf16[64,10,1]{2,0,1:T(8,128)(2,1)S(1)}, bf16[64,10,1]{2,0,1:T(8,128)(2,1)S(1)}, u32[]{:S(2)}, u32[]{:S(2)}) collective-permute-start(bf16[64,10,1]{2,0,1:T(8,128)(2,1)S(1)} %get-tuple-element.97), channel_id=1, source_target_pairs={{2,0},{0,2},{3,1},{1,3},{6,4},{4,6},{7,5},{5,7},{10,8},{8,10},{11,... | collective-permute-start | bytes 3848 | tf_op jit(solution)/shard_map/ppermute | solution.py:23
  58.6 11.5 %all-to-all-start.3 = ((bf16[4,2,64,128]{3,2,1,0:T(8,128)(2,1)}), bf16[4,2,64,128]{3,2,1,0:T(8,128)(2,1)S(1)}, u32[]{:S(2)}, u32[]{:S(2)}) async-start(bf16[4,2,64,128]{3,2,1,0:T(8,128)(2,1)} %bitcast.17), calls=%async_computation.3 | async-start | bytes 262144 | tf_op jit(solution)/shard_map/all_to_all | solution.py:132
  70.1 23.0 %all-to-all-start.2 = ((bf16[4,2,128,128]{3,2,1,0:T(8,128)(2,1)}), bf16[4,2,128,128]{3,2,1,0:T(8,128)(2,1)S(1)}, u32[]{:S(2)}, u32[]{:S(2)}) async-start(bf16[4,2,128,128]{3,2,1,0:T(8,128)(2,1)} %broadcast_select_fusion), calls=%async_computation.2 | async-start | bytes 524288 | tf_op jit(solution)/shard_map/all_to_all | solution.py:131
  101.0 5.8 %collective-permute-start.8 = (bf16[64,1,256]{2,0,1:T(8,128)(2,1)S(1)}, bf16[64,1,256]{2,0,1:T(8,128)(2,1)S(1)}, u32[]{:S(2)}, u32[]{:S(2)}) collective-permute-start(bf16[64,1,256]{2,0,1:T(8,128)(2,1)S(1)} %get-tuple-element.114), channel_id=1, source_target_pairs={{0,4},{4,8},{8,12},{12,0},{1,5},{5,9},{9,13},{13,1},{2,6},{6,10},{... | collective-permute-start | bytes 98312 | tf_op jit(solution)/shard_map/ppermute | solution.py:22
  103.1 4.0 %collective-permute-start.9 = (bf16[64,1,256]{2,0,1:T(8,128)(2,1)S(1)}, bf16[64,1,256]{2,0,1:T(8,128)(2,1)S(1)}, u32[]{:S(2)}, u32[]{:S(2)}) collective-permute-start(bf16[64,1,256]{2,0,1:T(8,128)(2,1)S(1)} %get-tuple-element.115), channel_id=1, source_target_pairs={{4,0},{8,4},{12,8},{0,12},{5,1},{9,5},{13,9},{1,13},{6,2},{10,6},{... | collective-permute-start | bytes 98312 | tf_op jit(solution)/shard_map/ppermute | solution.py:23
  107.3 6.3 %collective-permute-start.10 = (bf16[64,10,1]{2,0,1:T(8,128)(2,1)S(1)}, bf16[64,10,1]{2,0,1:T(8,128)(2,1)S(1)}, u32[]{:S(2)}, u32[]{:S(2)}) collective-permute-start(bf16[64,10,1]{2,0,1:T(8,128)(2,1)S(1)} %get-tuple-element.94), channel_id=1, source_target_pairs={{0,2},{2,0},{1,3},{3,1},{4,6},{6,4},{5,7},{7,5},{8,10},{10,8},{9,1... | collective-permute-start | bytes 3848 | tf_op jit(solution)/shard_map/ppermute | solution.py:22
  108.9 6.4 %collective-permute-start.11 = (bf16[64,10,1]{2,0,1:T(8,128)(2,1)S(1)}, bf16[64,10,1]{2,0,1:T(8,128)(2,1)S(1)}, u32[]{:S(2)}, u32[]{:S(2)}) collective-permute-start(bf16[64,10,1]{2,0,1:T(8,128)(2,1)S(1)} %get-tuple-element.95), channel_id=1, source_target_pairs={{2,0},{0,2},{3,1},{1,3},{6,4},{4,6},{7,5},{5,7},{10,8},{8,10},{11,... | collective-permute-start | bytes 3848 | tf_op jit(solution)/shard_map/ppermute | solution.py:23
  121.3 5.8 %collective-permute-start.12 = (bf16[64,1,256]{2,0,1:T(8,128)(2,1)S(1)}, bf16[64,1,256]{2,0,1:T(8,128)(2,1)S(1)}, u32[]{:S(2)}, u32[]{:S(2)}) collective-permute-start(bf16[64,1,256]{2,0,1:T(8,128)(2,1)S(1)} %get-tuple-element.112), channel_id=1, source_target_pairs={{0,4},{4,8},{8,12},{12,0},{1,5},{5,9},{9,13},{13,1},{2,6},{6,10},{... | collective-permute-start | bytes 98312 | tf_op jit(solution)/shard_map/ppermute | solution.py:22
  122.8 4.4 %collective-permute-start.13 = (bf16[64,1,256]{2,0,1:T(8,128)(2,1)S(1)}, bf16[64,1,256]{2,0,1:T(8,128)(2,1)S(1)}, u32[]{:S(2)}, u32[]{:S(2)}) collective-permute-start(bf16[64,1,256]{2,0,1:T(8,128)(2,1)S(1)} %get-tuple-element.113), channel_id=1, source_target_pairs={{4,0},{8,4},{12,8},{0,12},{5,1},{9,5},{13,9},{1,13},{6,2},{10,6},{... | collective-permute-start | bytes 98312 | tf_op jit(solution)/shard_map/ppermute | solution.py:23
  127.4 7.1 %collective-permute-start.14 = (bf16[64,10,1]{2,0,1:T(8,128)(2,1)S(1)}, bf16[64,10,1]{2,0,1:T(8,128)(2,1)S(1)}, u32[]{:S(2)}, u32[]{:S(2)}) collective-permute-start(bf16[64,10,1]{2,0,1:T(8,128)(2,1)S(1)} %get-tuple-element.92), channel_id=1, source_target_pairs={{0,2},{2,0},{1,3},{3,1},{4,6},{6,4},{5,7},{7,5},{8,10},{10,8},{9,1... | collective-permute-start | bytes 3848 | tf_op jit(solution)/shard_map/ppermute | solution.py:22
  129.0 7.2 %collective-permute-start.15 = (bf16[64,10,1]{2,0,1:T(8,128)(2,1)S(1)}, bf16[64,10,1]{2,0,1:T(8,128)(2,1)S(1)}, u32[]{:S(2)}, u32[]{:S(2)}) collective-permute-start(bf16[64,10,1]{2,0,1:T(8,128)(2,1)S(1)} %get-tuple-element.93), channel_id=1, source_target_pairs={{2,0},{0,2},{3,1},{1,3},{6,4},{4,6},{7,5},{5,7},{10,8},{8,10},{11,... | collective-permute-start | bytes 3848 | tf_op jit(solution)/shard_map/ppermute | solution.py:23
  129.5 13.2 %all-to-all-start.5 = ((bf16[4,2,64,128]{3,2,1,0:T(8,128)(2,1)}), bf16[4,2,64,128]{3,2,1,0:T(8,128)(2,1)S(1)}, u32[]{:S(2)}, u32[]{:S(2)}) async-start(bf16[4,2,64,128]{3,2,1,0:T(8,128)(2,1)} %bitcast.51), calls=%async_computation.5 | async-start | bytes 262144 | tf_op jit(solution)/shard_map/all_to_all | solution.py:146
  (9 other events, 74.0 us)
where the time goes:
time: 145 us; the launch traced here: 144 us
  starting transfers between devices  51.6 us (36%)
  local copies, waits for them, and re-layouts  35.9 us (25%)
  waiting for transfers between devices  24.5 us (17%)
  other arithmetic  13.2 us (9%)
  blocking collectives  10 us (7%)
  matrix products  7.13 us (5%)
    gather x48, local copies, waits for them, and re-layouts  17.9 us
    ppermute x8, starting transfers between devices, extended(): before = lax.ppermute(last, axis, up)  14.8 us
    ppermute x8, waiting for transfers between devices, extended(): before = lax.ppermute(last, axis, up)  13.1 us
    ppermute x8, starting transfers between devices, extended(): after = lax.ppermute(initial, axis, down)  10.6 us
    all_gather x4, blocking collectives, convolve(): lax.all_gather(padded, 'ch', axis=0, tiled=True)  10 us
    ppermute x8, waiting for transfers between devices, extended(): after = lax.ppermute(initial, axis, down)  7.17 us
    unnamed x5, other arithmetic  6.44 us
    dot_general x12, matrix products, apply_taps(): jnp.einsum('oi,ihw->ohw', row_kernel, stacked, preferred_element_type=jnp...  5.9 us
  transfers between devices with their start and end apart: 22, of which 13 were waited for; matrix products, arithmetic and copies ran while one was open for 28% of the time, Pallas kernels for 0%

commit v1 on v0

--- a/solution.py
+++ b/solution.py
@@ -10,6 +10,29 @@
 keep_rate = 0.6
 blend_rate = 0.4
 guide_rate = 0.3
+
+
+def split_up(x, dim, peers):
+    dims = x.shape
+    tiles = x.reshape(*dims[:dim], peers, dims[dim] // peers, *dims[dim + 1 :])
+    return jnp.moveaxis(tiles, dim, 0)
+
+
+def laid_out(blocks, dim):
+    dims = list(blocks.shape[1:])
+    dims[dim] *= blocks.shape[0]
+    return jnp.moveaxis(blocks, 0, dim).reshape(dims)
+
+
+def pairwise_exchange(x, axis, split_dim, concat_dim):
+    size, mine = (lax.axis_size(axis), lax.axis_index(axis))
+    blocks = split_up(x, split_dim, size)
+    done = [blocks[mine]]
+    for hop in range(1, size):
+        sent = blocks[mine ^ hop]
+        done.append(lax.ppermute(sent, axis, [(i, i ^ hop) for i in range(size)]))
+    blocks = jnp.stack(done)[mine ^ jnp.arange(size)]
+    return laid_out(blocks, concat_dim)
 
 
 def extended(shard, sides, width):
@@ -131,7 +154,7 @@
         lax.all_to_all(weights_out, "lat", split_axis=0, concat_axis=0, tiled=True),
         lax.all_to_all(values_out, "lat", split_axis=0, concat_axis=0, tiled=True),
         lax.all_to_all(scale_out, "lat", split_axis=0, concat_axis=0, tiled=True),
-        lax.all_to_all(rows_out, "lat", split_axis=0, concat_axis=0, tiled=True),
+        pairwise_exchange(rows_out, "lat", 0, 0),
         lax.all_to_all(cols_out, "lat", split_axis=0, concat_axis=0, tiled=True),
     )
     weights_in = arrived[0].reshape(slots, OBS, PH * PW)

time: 145 us -> 142 us (0.979)
  waiting for transfers between devices: 24.5 us -> 20.8 us
    all_to_all x1 -> x0, starting transfers between devices: 5.06 us -> none  [observe(): lax.all_to_all(rows_out, 'lat', split_axis=0, concat_axis=0, tiled=True)]
    ppermute x0 -> x3, starting transfers between devices: none -> 4.44 us  [pairwise_exchange(): done.append(lax.ppermute(sent, axis, [(i, i ^ hop) for i in range(size)]))]
    all_to_all x1 -> x0, waiting for transfers between devices: 4.16 us -> none  [observe(): lax.all_to_all(rows_out, 'lat', split_axis=0, concat_axis=0, tiled=True)]
    all_to_all x1, starting transfers between devices: 3.24 us -> 5.06 us  [observe(): lax.all_to_all(scale_out, 'lat', split_axis=0, concat_axis=0, tiled=True)]
    gather x48 -> x49, local copies, waits for them, and re-layouts: 17.9 us -> 18.5 us
  transfers between devices with their start and end apart: 22 -> 24, of which waited for: 13 -> 12; matrix products, arithmetic and copies ran while one was open for 28% -> 29% of each run, Pallas kernels for 0% -> 0%
where the time goes in v1:
time: 142 us; the launch traced here: 141 us
  starting transfers between devices  52.8 us (37%)
  local copies, waits for them, and re-layouts  35.9 us (25%)
  waiting for transfers between devices  20.8 us (15%)
  other arithmetic  12.5 us (9%)
  blocking collectives  10 us (7%)
  matrix products  7.12 us (5%)
    gather x48, local copies, waits for them, and re-layouts  17.9 us
    ppermute x8, starting transfers between devices, extended(): before = lax.ppermute(last, axis, up)  14.7 us
    ppermute x8, waiting for transfers between devices, extended(): before = lax.ppermute(last, axis, up)  13.5 us
    ppermute x8, starting transfers between devices, extended(): after = lax.ppermute(initial, axis, down)  10.7 us
    all_gather x4, blocking collectives, convolve(): lax.all_gather(padded, 'ch', axis=0, tiled=True)  10 us
    ppermute x8, waiting for transfers between devices, extended(): after = lax.ppermute(initial, axis, down)  7.23 us
    unnamed x5, other arithmetic  6.44 us
    dot_general x12, matrix products, apply_taps(): jnp.einsum('oi,ihw->ohw', row_kernel, stacked, preferred_element_type=jnp...  5.89 us
  transfers between devices with their start and end apart: 24, of which 12 were waited for; matrix products, arithmetic and copies ran while one was open for 29% of the time, Pallas kernels for 0%

profile of v1, /device:TPU:0, one launch (start us, length us, event | category | flops | bytes accessed | tf_op | source)
XLA Modules:
  0.0 140.8 jit_solution(1604121698799299416)
XLA Ops:
  1.9 3.1 %collective-permute-start = (bf16[64,1,256]{2,0,1:T(8,128)(2,1)S(1)}, bf16[64,1,256]{2,0,1:T(8,128)(2,1)S(1)}, u32[]{:S(2)}, u32[]{:S(2)}) collective-permute-start(bf16[64,1,256]{2,0,1:T(8,128)(2,1)S(1)} %copy.206), channel_id=1, source_target_pairs={{0,4},{4,8},{8,12},{12,0},{1,5},{5,9},{9,13},{13,1},{2,6},{6,10},{... | collective-permute-start | bytes 98312 | tf_op jit(solution)/shard_map/ppermute | solution.py:45
  5.0 2.1 %collective-permute-start.1 = (bf16[64,1,256]{2,0,1:T(8,128)(2,1)S(1)}, bf16[64,1,256]{2,0,1:T(8,128)(2,1)S(1)}, u32[]{:S(2)}, u32[]{:S(2)}) collective-permute-start(bf16[64,1,256]{2,0,1:T(8,128)(2,1)S(1)} %copy.207), channel_id=1, source_target_pairs={{4,0},{8,4},{12,8},{0,12},{5,1},{9,5},{13,9},{1,13},{6,2},{10,6},{... | collective-permute-start | bytes 98312 | tf_op jit(solution)/shard_map/ppermute | solution.py:46
  11.5 2.5 %collective-permute-start.9 = (s32[1,2]{1,0:T(1,128)S(1)}, s32[1,2]{1,0:T(1,128)S(1)}, u32[]{:S(2)}, u32[]{:S(2)}) collective-permute-start(s32[1,2]{1,0:T(1,128)S(1)} %get-tuple-element.122), channel_id=1, source_target_pairs={{0,8},{4,12},{8,0},{12,4},{1,9},{5,13},{9,1},{13,5},{2,10},{6,14},... | collective-permute-start | bytes 32 | tf_op jit(solution)/shard_map/ppermute | solution.py:33
  14.0 1.9 %collective-permute-start.10 = (s32[1,2]{1,0:T(1,128)S(1)}, s32[1,2]{1,0:T(1,128)S(1)}, u32[]{:S(2)}, u32[]{:S(2)}) collective-permute-start(s32[1,2]{1,0:T(1,128)S(1)} %get-tuple-element.121), channel_id=1, source_target_pairs={{0,12},{4,8},{8,4},{12,0},{1,13},{5,9},{9,5},{13,1},{2,14},{6,10},... | collective-permute-start | bytes 32 | tf_op jit(solution)/shard_map/ppermute | solution.py:33
  17.2 3.2 %all-to-all-start = ((s32[4,1,2]{2,1,0:T(1,128)}), s32[4,1,2]{2,1,0:T(1,128)S(1)}, u32[]{:S(2)}, u32[]{:S(2)}) async-start(s32[4,1,2]{2,1,0:T(1,128)} %bitcast.23), calls=%async_computation | async-start | bytes 4096 | tf_op jit(solution)/shard_map/all_to_all | solution.py:158
  26.4 5.1 %all-to-all-start.3 = ((bf16[4,2,128]{2,1,0:T(2,128)(2,1)}), bf16[4,2,128]{2,1,0:T(2,128)(2,1)S(1)}, u32[]{:S(2)}, u32[]{:S(2)}) async-start(bf16[4,2,128]{2,1,0:T(2,128)(2,1)} %broadcast_select_fusion.2), calls=%async_computation.3 | async-start | bytes 4096 | tf_op jit(solution)/shard_map/all_to_all | solution.py:156
  35.4 3.9 %collective-permute-done.2 = bf16[64,10,1]{2,0,1:T(8,128)(2,1)S(1)} collective-permute-done((bf16[64,10,1]{2,0,1:T(8,128)(2,1)S(1)}, bf16[64,10,1]{2,0,1:T(8,128)(2,1)S(1)}, u32[]{:S(2)}, u32[]{:S(2)}) %collective-permute-start.2) | collective-permute-done | bytes 1312 | tf_op jit(solution)/shard_map/ppermute | solution.py:45
  39.3 1.8 %collective-permute-done.3 = bf16[64,10,1]{2,0,1:T(8,128)(2,1)S(1)} collective-permute-done((bf16[64,10,1]{2,0,1:T(8,128)(2,1)S(1)}, bf16[64,10,1]{2,0,1:T(8,128)(2,1)S(1)}, u32[]{:S(2)}, u32[]{:S(2)}) %collective-permute-start.3) | collective-permute-done | bytes 1312 | tf_op jit(solution)/shard_map/ppermute | solution.py:46
  41.4 2.5 %all_gather.12 = bf16[128,10,258]{2,0,1:T(8,128)(2,1)S(1)} all-gather(bf16[64,10,258]{2,0,1:T(8,128)(2,1)S(1)} %maximum_select_fusion), channel_id=1, replica_groups=mesh['grp'=2,'lat'=4,'lon'=2,'ch'=2] {'ch'}, dimensions={0}, use_global_device_ids=true | all-gather | bytes 990720 | tf_op jit(solution)/shard_map/all_gather | solution.py:85
  48.8 2.1 %collective-permute-start.5 = (bf16[64,1,256]{2,0,1:T(8,128)(2,1)S(1)}, bf16[64,1,256]{2,0,1:T(8,128)(2,1)S(1)}, u32[]{:S(2)}, u32[]{:S(2)}) collective-permute-start(bf16[64,1,256]{2,0,1:T(8,128)(2,1)S(1)} %get-tuple-element.117), channel_id=1, source_target_pairs={{4,0},{8,4},{12,8},{0,12},{5,1},{9,5},{13,9},{1,13},{6,2},{10,6},{... | collective-permute-start | bytes 98312 | tf_op jit(solution)/shard_map/ppermute | solution.py:46
  50.9 2.0 %collective-permute-done.4 = bf16[64,1,256]{2,0,1:T(8,128)(2,1)S(1)} collective-permute-done((bf16[64,1,256]{2,0,1:T(8,128)(2,1)S(1)}, bf16[64,1,256]{2,0,1:T(8,128)(2,1)S(1)}, u32[]{:S(2)}, u32[]{:S(2)}) %collective-permute-start.4) | collective-permute-done | bytes 32800 | tf_op jit(solution)/shard_map/ppermute | solution.py:45
  55.5 4.8 %all-to-all-start.2 = ((bf16[4,2,64,128]{3,2,1,0:T(8,128)(2,1)}), bf16[4,2,64,128]{3,2,1,0:T(8,128)(2,1)S(1)}, u32[]{:S(2)}, u32[]{:S(2)}) async-start(bf16[4,2,64,128]{3,2,1,0:T(8,128)(2,1)} %bitcast.27), calls=%async_computation.2 | async-start | bytes 262144 | tf_op jit(solution)/shard_map/all_to_all | solution.py:155
  62.0 2.5 %all_gather.13 = bf16[128,10,258]{2,0,1:T(8,128)(2,1)S(1)} all-gather(bf16[64,10,258]{2,0,1:T(8,128)(2,1)S(1)} %maximum_select_fusion.1), channel_id=1, replica_groups=mesh['grp'=2,'lat'=4,'lon'=2,'ch'=2] {'ch'}, dimensions={0}, use_global_device_ids=true | all-gather | bytes 990720 | tf_op jit(solution)/shard_map/all_gather | solution.py:85
  66.9 4.9 %all-to-all-start.1 = ((bf16[4,2,128,128]{3,2,1,0:T(8,128)(2,1)}), bf16[4,2,128,128]{3,2,1,0:T(8,128)(2,1)S(1)}, u32[]{:S(2)}, u32[]{:S(2)}) async-start(bf16[4,2,128,128]{3,2,1,0:T(8,128)(2,1)} %broadcast_select_fusion), calls=%async_computation.1 | async-start | bytes 524288 | tf_op jit(solution)/shard_map/all_to_all | solution.py:154
  71.8 18.2 %while.1 = (s32[]{:T(128)}, bf16[64,8,256]{2,0,1:T(8,128)(2,1)S(1)}, s32[8,3]{0,1:T(4,128)S(1)}, bf16[8,64,4,32]{1,3,2,0:T(8,128)(2,1)S(1)}, s32[]{:T(128)}) while((s32[]{:T(128)}, bf16[64,8,256]{2,0,1:T(8,128)(2,1)S(1)}, s32[8,3]{0,1:T(4,128)S(1)}, bf16[8,64,4,32]{1,3,2,0:T(8,128)(2,1)S(1)}, s32[]{:T(128)}) %tuple.90), condition=%wide.while_cond, body=%wide.while_body.sunk | while | flops 2 | bytes 163957 | solution.py:101
  91.2 6.3 %scatter_custom_fusion.1 = f32[64,2048]{0,1:T(8,128)S(1)} fusion(s32[1024]{0:T(1024)S(1)} %reshape.354, f32[1024,64]{1,0:T(8,128)S(1)} %bitcast.145, f32[]{:T(128)} %constant.31.clone.1), kind=kCustom, calls=%fused_computation.105 | custom fusion | flops 65536 | bytes 524292
  97.9 2.1 %collective-permute-start.11 = (bf16[64,1,256]{2,0,1:T(8,128)(2,1)S(1)}, bf16[64,1,256]{2,0,1:T(8,128)(2,1)S(1)}, u32[]{:S(2)}, u32[]{:S(2)}) collective-permute-start(bf16[64,1,256]{2,0,1:T(8,128)(2,1)S(1)} %get-tuple-element.114), channel_id=1, source_target_pairs={{0,4},{4,8},{8,12},{12,0},{1,5},{5,9},{9,13},{13,1},{2,6},{6,10},{... | collective-permute-start | bytes 98312 | tf_op jit(solution)/shard_map/ppermute | solution.py:45
  100.0 2.0 %collective-permute-start.12 = (bf16[64,1,256]{2,0,1:T(8,128)(2,1)S(1)}, bf16[64,1,256]{2,0,1:T(8,128)(2,1)S(1)}, u32[]{:S(2)}, u32[]{:S(2)}) collective-permute-start(bf16[64,1,256]{2,0,1:T(8,128)(2,1)S(1)} %get-tuple-element.115), channel_id=1, source_target_pairs={{4,0},{8,4},{12,8},{0,12},{5,1},{9,5},{13,9},{1,13},{6,2},{10,6},{... | collective-permute-start | bytes 98312 | tf_op jit(solution)/shard_map/ppermute | solution.py:46
  106.3 4.2 %collective-permute-done.13 = bf16[64,10,1]{2,0,1:T(8,128)(2,1)S(1)} collective-permute-done((bf16[64,10,1]{2,0,1:T(8,128)(2,1)S(1)}, bf16[64,10,1]{2,0,1:T(8,128)(2,1)S(1)}, u32[]{:S(2)}, u32[]{:S(2)}) %collective-permute-start.13) | collective-permute-done | bytes 1312 | tf_op jit(solution)/shard_map/ppermute | solution.py:45
  112.6 2.5 %all_gather.14 = bf16[128,10,258]{2,0,1:T(8,128)(2,1)S(1)} all-gather(bf16[64,10,258]{2,0,1:T(8,128)(2,1)S(1)} %maximum_select_fusion.2), channel_id=1, replica_groups=mesh['grp'=2,'lat'=4,'lon'=2,'ch'=2] {'ch'}, dimensions={0}, use_global_device_ids=true | all-gather | bytes 990720 | tf_op jit(solution)/shard_map/all_gather | solution.py:85
  119.7 2.4 %collective-permute-start.16 = (bf16[64,1,256]{2,0,1:T(8,128)(2,1)S(1)}, bf16[64,1,256]{2,0,1:T(8,128)(2,1)S(1)}, u32[]{:S(2)}, u32[]{:S(2)}) collective-permute-start(bf16[64,1,256]{2,0,1:T(8,128)(2,1)S(1)} %get-tuple-element.113), channel_id=1, source_target_pairs={{4,0},{8,4},{12,8},{0,12},{5,1},{9,5},{13,9},{1,13},{6,2},{10,6},{... | collective-permute-start | bytes 98312 | tf_op jit(solution)/shard_map/ppermute | solution.py:46
  122.2 1.9 %collective-permute-done.15 = bf16[64,1,256]{2,0,1:T(8,128)(2,1)S(1)} collective-permute-done((bf16[64,1,256]{2,0,1:T(8,128)(2,1)S(1)}, bf16[64,1,256]{2,0,1:T(8,128)(2,1)S(1)}, u32[]{:S(2)}, u32[]{:S(2)}) %collective-permute-start.15) | collective-permute-done | bytes 32800 | tf_op jit(solution)/shard_map/ppermute | solution.py:45
  126.4 5.0 %all-to-all-start.4 = ((bf16[4,2,64,128]{3,2,1,0:T(8,128)(2,1)}), bf16[4,2,64,128]{3,2,1,0:T(8,128)(2,1)S(1)}, u32[]{:S(2)}, u32[]{:S(2)}) async-start(bf16[4,2,64,128]{3,2,1,0:T(8,128)(2,1)} %bitcast.61), calls=%async_computation.4 | async-start | bytes 262144 | tf_op jit(solution)/shard_map/all_to_all | solution.py:169
  133.5 2.5 %all_gather.15 = bf16[128,10,258]{2,0,1:T(8,128)(2,1)S(1)} all-gather(bf16[64,10,258]{2,0,1:T(8,128)(2,1)S(1)} %maximum_select_fusion.3), channel_id=1, replica_groups=mesh['grp'=2,'lat'=4,'lon'=2,'ch'=2] {'ch'}, dimensions={0}, use_global_device_ids=true | all-gather | bytes 990720 | tf_op jit(solution)/shard_map/all_gather | solution.py:85
  (208 shorter events, 68.1 us)
Async XLA Ops:
  1.9 31.1 %collective-permute-start = (bf16[64,1,256]{2,0,1:T(8,128)(2,1)S(1)}, bf16[64,1,256]{2,0,1:T(8,128)(2,1)S(1)}, u32[]{:S(2)}, u32[]{:S(2)}) collective-permute-start(bf16[64,1,256]{2,0,1:T(8,128)(2,1)S(1)} %copy.206), channel_id=1, source_target_pairs={{0,4},{4,8},{8,12},{12,0},{1,5},{5,9},{9,13},{13,1},{2,6},{6,10},{... | collective-permute-start | bytes 98312 | tf_op jit(solution)/shard_map/ppermute | solution.py:45
  5.0 28.1 %collective-permute-start.1 = (bf16[64,1,256]{2,0,1:T(8,128)(2,1)S(1)}, bf16[64,1,256]{2,0,1:T(8,128)(2,1)S(1)}, u32[]{:S(2)}, u32[]{:S(2)}) collective-permute-start(bf16[64,1,256]{2,0,1:T(8,128)(2,1)S(1)} %copy.207), channel_id=1, source_target_pairs={{4,0},{8,4},{12,8},{0,12},{5,1},{9,5},{13,9},{1,13},{6,2},{10,6},{... | collective-permute-start | bytes 98312 | tf_op jit(solution)/shard_map/ppermute | solution.py:46
  11.4 14.2 %collective-permute-start.8 = (s32[1,2]{1,0:T(1,128)S(1)}, s32[1,2]{1,0:T(1,128)S(1)}, u32[]{:S(2)}, u32[]{:S(2)}) collective-permute-start(s32[1,2]{1,0:T(1,128)S(1)} %get-tuple-element.123), channel_id=1, source_target_pairs={{0,4},{4,0},{8,12},{12,8},{1,5},{5,1},{9,13},{13,9},{2,6},{6,2},{1... | collective-permute-start | bytes 32 | tf_op jit(solution)/shard_map/ppermute | solution.py:33
  11.5 14.1 %collective-permute-start.9 = (s32[1,2]{1,0:T(1,128)S(1)}, s32[1,2]{1,0:T(1,128)S(1)}, u32[]{:S(2)}, u32[]{:S(2)}) collective-permute-start(s32[1,2]{1,0:T(1,128)S(1)} %get-tuple-element.122), channel_id=1, source_target_pairs={{0,8},{4,12},{8,0},{12,4},{1,9},{5,13},{9,1},{13,5},{2,10},{6,14},... | collective-permute-start | bytes 32 | tf_op jit(solution)/shard_map/ppermute | solution.py:33
  14.0 11.6 %collective-permute-start.10 = (s32[1,2]{1,0:T(1,128)S(1)}, s32[1,2]{1,0:T(1,128)S(1)}, u32[]{:S(2)}, u32[]{:S(2)}) collective-permute-start(s32[1,2]{1,0:T(1,128)S(1)} %get-tuple-element.121), channel_id=1, source_target_pairs={{0,12},{4,8},{8,4},{12,0},{1,13},{5,9},{9,5},{13,1},{2,14},{6,10},... | collective-permute-start | bytes 32 | tf_op jit(solution)/shard_map/ppermute | solution.py:33
  17.2 9.2 %all-to-all-start = ((s32[4,1,2]{2,1,0:T(1,128)}), s32[4,1,2]{2,1,0:T(1,128)S(1)}, u32[]{:S(2)}, u32[]{:S(2)}) async-start(s32[4,1,2]{2,1,0:T(1,128)} %bitcast.23), calls=%async_computation | async-start | bytes 4096 | tf_op jit(solution)/shard_map/all_to_all | solution.py:158
  26.4 29.1 %all-to-all-start.3 = ((bf16[4,2,128]{2,1,0:T(2,128)(2,1)}), bf16[4,2,128]{2,1,0:T(2,128)(2,1)S(1)}, u32[]{:S(2)}, u32[]{:S(2)}) async-start(bf16[4,2,128]{2,1,0:T(2,128)(2,1)} %broadcast_select_fusion.2), calls=%async_computation.3 | async-start | bytes 4096 | tf_op jit(solution)/shard_map/all_to_all | solution.py:156
  33.2 6.1 %collective-permute-start.2 = (bf16[64,10,1]{2,0,1:T(8,128)(2,1)S(1)}, bf16[64,10,1]{2,0,1:T(8,128)(2,1)S(1)}, u32[]{:S(2)}, u32[]{:S(2)}) collective-permute-start(bf16[64,10,1]{2,0,1:T(8,128)(2,1)S(1)} %get-tuple-element.98), channel_id=1, source_target_pairs={{0,2},{2,0},{1,3},{3,1},{4,6},{6,4},{5,7},{7,5},{8,10},{10,8},{9,1... | collective-permute-start | bytes 3848 | tf_op jit(solution)/shard_map/ppermute | solution.py:45
  34.9 6.1 %collective-permute-start.3 = (bf16[64,10,1]{2,0,1:T(8,128)(2,1)S(1)}, bf16[64,10,1]{2,0,1:T(8,128)(2,1)S(1)}, u32[]{:S(2)}, u32[]{:S(2)}) collective-permute-start(bf16[64,10,1]{2,0,1:T(8,128)(2,1)S(1)} %get-tuple-element.99), channel_id=1, source_target_pairs={{2,0},{0,2},{3,1},{1,3},{6,4},{4,6},{7,5},{5,7},{10,8},{8,10},{11,... | collective-permute-start | bytes 3848 | tf_op jit(solution)/shard_map/ppermute | solution.py:46
  47.1 5.8 %collective-permute-start.4 = (bf16[64,1,256]{2,0,1:T(8,128)(2,1)S(1)}, bf16[64,1,256]{2,0,1:T(8,128)(2,1)S(1)}, u32[]{:S(2)}, u32[]{:S(2)}) collective-permute-start(bf16[64,1,256]{2,0,1:T(8,128)(2,1)S(1)} %get-tuple-element.116), channel_id=1, source_target_pairs={{0,4},{4,8},{8,12},{12,0},{1,5},{5,9},{9,13},{13,1},{2,6},{6,10},{... | collective-permute-start | bytes 98312 | tf_op jit(solution)/shard_map/ppermute | solution.py:45
  48.8 4.3 %collective-permute-start.5 = (bf16[64,1,256]{2,0,1:T(8,128)(2,1)S(1)}, bf16[64,1,256]{2,0,1:T(8,128)(2,1)S(1)}, u32[]{:S(2)}, u32[]{:S(2)}) collective-permute-start(bf16[64,1,256]{2,0,1:T(8,128)(2,1)S(1)} %get-tuple-element.117), channel_id=1, source_target_pairs={{4,0},{8,4},{12,8},{0,12},{5,1},{9,5},{13,9},{1,13},{6,2},{10,6},{... | collective-permute-start | bytes 98312 | tf_op jit(solution)/shard_map/ppermute | solution.py:46
  53.3 7.0 %collective-permute-start.6 = (bf16[64,10,1]{2,0,1:T(8,128)(2,1)S(1)}, bf16[64,10,1]{2,0,1:T(8,128)(2,1)S(1)}, u32[]{:S(2)}, u32[]{:S(2)}) collective-permute-start(bf16[64,10,1]{2,0,1:T(8,128)(2,1)S(1)} %get-tuple-element.96), channel_id=1, source_target_pairs={{0,2},{2,0},{1,3},{3,1},{4,6},{6,4},{5,7},{7,5},{8,10},{10,8},{9,1... | collective-permute-start | bytes 3848 | tf_op jit(solution)/shard_map/ppermute | solution.py:45
  54.8 6.8 %collective-permute-start.7 = (bf16[64,10,1]{2,0,1:T(8,128)(2,1)S(1)}, bf16[64,10,1]{2,0,1:T(8,128)(2,1)S(1)}, u32[]{:S(2)}, u32[]{:S(2)}) collective-permute-start(bf16[64,10,1]{2,0,1:T(8,128)(2,1)S(1)} %get-tuple-element.97), channel_id=1, source_target_pairs={{2,0},{0,2},{3,1},{1,3},{6,4},{4,6},{7,5},{5,7},{10,8},{8,10},{11,... | collective-permute-start | bytes 3848 | tf_op jit(solution)/shard_map/ppermute | solution.py:46
  55.5 11.5 %all-to-all-start.2 = ((bf16[4,2,64,128]{3,2,1,0:T(8,128)(2,1)}), bf16[4,2,64,128]{3,2,1,0:T(8,128)(2,1)S(1)}, u32[]{:S(2)}, u32[]{:S(2)}) async-start(bf16[4,2,64,128]{3,2,1,0:T(8,128)(2,1)} %bitcast.27), calls=%async_computation.2 | async-start | bytes 262144 | tf_op jit(solution)/shard_map/all_to_all | solution.py:155
  66.9 23.1 %all-to-all-start.1 = ((bf16[4,2,128,128]{3,2,1,0:T(8,128)(2,1)}), bf16[4,2,128,128]{3,2,1,0:T(8,128)(2,1)S(1)}, u32[]{:S(2)}, u32[]{:S(2)}) async-start(bf16[4,2,128,128]{3,2,1,0:T(8,128)(2,1)} %broadcast_select_fusion), calls=%async_computation.1 | async-start | bytes 524288 | tf_op jit(solution)/shard_map/all_to_all | solution.py:154
  97.9 5.8 %collective-permute-start.11 = (bf16[64,1,256]{2,0,1:T(8,128)(2,1)S(1)}, bf16[64,1,256]{2,0,1:T(8,128)(2,1)S(1)}, u32[]{:S(2)}, u32[]{:S(2)}) collective-permute-start(bf16[64,1,256]{2,0,1:T(8,128)(2,1)S(1)} %get-tuple-element.114), channel_id=1, source_target_pairs={{0,4},{4,8},{8,12},{12,0},{1,5},{5,9},{9,13},{13,1},{2,6},{6,10},{... | collective-permute-start | bytes 98312 | tf_op jit(solution)/shard_map/ppermute | solution.py:45
  100.0 4.0 %collective-permute-start.12 = (bf16[64,1,256]{2,0,1:T(8,128)(2,1)S(1)}, bf16[64,1,256]{2,0,1:T(8,128)(2,1)S(1)}, u32[]{:S(2)}, u32[]{:S(2)}) collective-permute-start(bf16[64,1,256]{2,0,1:T(8,128)(2,1)S(1)} %get-tuple-element.115), channel_id=1, source_target_pairs={{4,0},{8,4},{12,8},{0,12},{5,1},{9,5},{13,9},{1,13},{6,2},{10,6},{... | collective-permute-start | bytes 98312 | tf_op jit(solution)/shard_map/ppermute | solution.py:46
  104.2 6.3 %collective-permute-start.13 = (bf16[64,10,1]{2,0,1:T(8,128)(2,1)S(1)}, bf16[64,10,1]{2,0,1:T(8,128)(2,1)S(1)}, u32[]{:S(2)}, u32[]{:S(2)}) collective-permute-start(bf16[64,10,1]{2,0,1:T(8,128)(2,1)S(1)} %get-tuple-element.94), channel_id=1, source_target_pairs={{0,2},{2,0},{1,3},{3,1},{4,6},{6,4},{5,7},{7,5},{8,10},{10,8},{9,1... | collective-permute-start | bytes 3848 | tf_op jit(solution)/shard_map/ppermute | solution.py:45
  105.7 6.5 %collective-permute-start.14 = (bf16[64,10,1]{2,0,1:T(8,128)(2,1)S(1)}, bf16[64,10,1]{2,0,1:T(8,128)(2,1)S(1)}, u32[]{:S(2)}, u32[]{:S(2)}) collective-permute-start(bf16[64,10,1]{2,0,1:T(8,128)(2,1)S(1)} %get-tuple-element.95), channel_id=1, source_target_pairs={{2,0},{0,2},{3,1},{1,3},{6,4},{4,6},{7,5},{5,7},{10,8},{8,10},{11,... | collective-permute-start | bytes 3848 | tf_op jit(solution)/shard_map/ppermute | solution.py:46
  118.3 5.8 %collective-permute-start.15 = (bf16[64,1,256]{2,0,1:T(8,128)(2,1)S(1)}, bf16[64,1,256]{2,0,1:T(8,128)(2,1)S(1)}, u32[]{:S(2)}, u32[]{:S(2)}) collective-permute-start(bf16[64,1,256]{2,0,1:T(8,128)(2,1)S(1)} %get-tuple-element.112), channel_id=1, source_target_pairs={{0,4},{4,8},{8,12},{12,0},{1,5},{5,9},{9,13},{13,1},{2,6},{6,10},{... | collective-permute-start | bytes 98312 | tf_op jit(solution)/shard_map/ppermute | solution.py:45
  119.7 4.4 %collective-permute-start.16 = (bf16[64,1,256]{2,0,1:T(8,128)(2,1)S(1)}, bf16[64,1,256]{2,0,1:T(8,128)(2,1)S(1)}, u32[]{:S(2)}, u32[]{:S(2)}) collective-permute-start(bf16[64,1,256]{2,0,1:T(8,128)(2,1)S(1)} %get-tuple-element.113), channel_id=1, source_target_pairs={{4,0},{8,4},{12,8},{0,12},{5,1},{9,5},{13,9},{1,13},{6,2},{10,6},{... | collective-permute-start | bytes 98312 | tf_op jit(solution)/shard_map/ppermute | solution.py:46
  124.3 7.1 %collective-permute-start.17 = (bf16[64,10,1]{2,0,1:T(8,128)(2,1)S(1)}, bf16[64,10,1]{2,0,1:T(8,128)(2,1)S(1)}, u32[]{:S(2)}, u32[]{:S(2)}) collective-permute-start(bf16[64,10,1]{2,0,1:T(8,128)(2,1)S(1)} %get-tuple-element.92), channel_id=1, source_target_pairs={{0,2},{2,0},{1,3},{3,1},{4,6},{6,4},{5,7},{7,5},{8,10},{10,8},{9,1... | collective-permute-start | bytes 3848 | tf_op jit(solution)/shard_map/ppermute | solution.py:45
  125.8 7.3 %collective-permute-start.18 = (bf16[64,10,1]{2,0,1:T(8,128)(2,1)S(1)}, bf16[64,10,1]{2,0,1:T(8,128)(2,1)S(1)}, u32[]{:S(2)}, u32[]{:S(2)}) collective-permute-start(bf16[64,10,1]{2,0,1:T(8,128)(2,1)S(1)} %get-tuple-element.93), channel_id=1, source_target_pairs={{2,0},{0,2},{3,1},{1,3},{6,4},{4,6},{7,5},{5,7},{10,8},{8,10},{11,... | collective-permute-start | bytes 3848 | tf_op jit(solution)/shard_map/ppermute | solution.py:46
  126.4 13.2 %all-to-all-start.4 = ((bf16[4,2,64,128]{3,2,1,0:T(8,128)(2,1)}), bf16[4,2,64,128]{3,2,1,0:T(8,128)(2,1)S(1)}, u32[]{:S(2)}, u32[]{:S(2)}) async-start(bf16[4,2,64,128]{3,2,1,0:T(8,128)(2,1)} %bitcast.61), calls=%async_computation.4 | async-start | bytes 262144 | tf_op jit(solution)/shard_map/all_to_all | solution.py:169
  (11 other events, 115.8 us)
